TPU v7x, 32 devices: a whole 2x2x4 slice. The times are simulated.
32 devices in a mesh: elem: 8 (over z, core), lev: 4 (over y, x).
Axes of the slice: x: 2, y: 2, z: 4, core: 2. Of those that a mesh axis runs over, the one named last changes fastest.
Arguments:
- tracers: float32 [512, 16, 640], P('elem', 'lev'), may hold values from 0.1 to 120, as said below
- ref_index: int32 [512, 16], P('elem'), may hold values from 0 to 63
- requests: int32 [8, 2, 16], P('elem'), may hold values from -1 to 63, as said below
- source: int32 [512], P('elem'), may hold values from 0 to 95, as said below
- target_mean: float32 [40], replicated, may hold values from 0.5 to 5
Outputs:
- transported: float32 [512, 16, 640], P('elem', 'lev')
Inputs may be any that keep to these rules, and one draw needn't show every extreme that they name: Row 0 of requests[d] holds distinct element indices of block d - 1 (wrapping), row 1 of block d + 1; the valid entries come first and the rest are -1; every row holds 1 to 16 valid entries and some row holds exactly 16. `source`: every slot names an own element (below 64) or a valid entry of the block's requests: 64 + k for row 0, 80 + k for row 1. `tracers`: all entries are positive.
All inputs are finite; a program needn't handle non-finite values.
Results may differ from a plain program's by a relative error of at most 0.0003.
Values sent between devices are 32-bit elements; how exact they have to be, the bound alone decides.
A program may use at most 64 MiB of HBM per device.

v0:
```python
import math
import jax
import jax.numpy as jnp
from jax import lax
from jax.sharding import PartitionSpec as P

NPTS = 16
REFS = 64


def with_halo(cells, sides, width):
    for axis, dim in sides:
        count = lax.axis_size(axis)
        head = lax.slice_in_dim(cells, 0, width, axis=dim)
        tail = lax.slice_in_dim(cells, cells.shape[dim] - width, cells.shape[dim], axis=dim)
        cells = jnp.concatenate(
            [
                lax.ppermute(tail, axis, [(i, (i + 1) % count) for i in range(count)]),
                cells,
                lax.ppermute(head, axis, [((i + 1) % count, i) for i in range(count)]),
            ],
            axis=dim,
        )
    return cells


def lagrange_table():
    side = math.isqrt(REFS)
    gll_nodes = [-1.0, -math.sqrt(0.2), math.sqrt(0.2), 1.0]
    points = -1.0 + 2.0 * jnp.arange(side, dtype=jnp.float32) / (side - 1)
    columns = []
    for which in range(4):
        basis = jnp.ones((side,), jnp.float32)
        for other in range(4):
            if other != which:
                basis = basis * (points - gll_nodes[other]) / (gll_nodes[which] - gll_nodes[other])
        columns.append(basis)
    one_dim = jnp.stack(columns, axis=1)
    return (one_dim[:, None, :, None] * one_dim[None, :, None, :]).reshape(side * side, 16)


def quadrature():
    edge = jnp.array([1.0 / 6.0, 5.0 / 6.0, 5.0 / 6.0, 1.0 / 6.0], jnp.float32)
    return (edge[:, None] * edge[None, :]).reshape(16)


def interpolate(source_rows, ref_index):
    elem_count, levels, width = source_rows.shape
    onehot = (ref_index[:, :, None] == jnp.arange(REFS, dtype=jnp.int32)[None, None, :]).astype(
        jnp.float32
    )
    matrix = jnp.einsum("epr,rn->epn", onehot, lagrange_table(), precision=lax.Precision.HIGHEST)
    values = source_rows.reshape(elem_count, levels * (width // 16), 16)
    result = jnp.einsum("epn,ecn->ecp", matrix, values, precision=lax.Precision.HIGHEST)
    lowest = jnp.min(values, axis=2, keepdims=True)
    highest = jnp.max(values, axis=2, keepdims=True)
    result = jnp.minimum(jnp.maximum(result, lowest), highest)
    return result.reshape(elem_count, levels, width)


def per_device(tracers, ref_index, requests, source, target_mean):
    elem_count, levels, width = tracers.shape
    beside_all = with_halo(tracers, (("elem", 0),), elem_count)
    own_pos = jnp.arange(elem_count, 2 * elem_count, dtype=jnp.int32)
    left_pos = jnp.maximum(requests[0, 0], 0)
    right_pos = 2 * elem_count + jnp.maximum(requests[0, 1], 0)
    slot_pos = jnp.concatenate([own_pos, left_pos, right_pos])
    source_rows = beside_all[slot_pos[source]]
    clipped = interpolate(source_rows, ref_index)
    tracer_count = width // NPTS
    shaped = clipped.reshape(elem_count, levels, tracer_count, NPTS)
    local_mass = jnp.einsum("eltn,n->t", shaped, quadrature(), precision=lax.Precision.HIGHEST)
    column_mass = lax.psum(local_mass, "lev")
    global_mass = lax.psum(column_mass, "elem")
    whole_weight = 4.0 * elem_count * lax.axis_size("elem") * levels * lax.axis_size("lev")
    factor = target_mean * whole_weight / global_mass
    return (shaped * factor[None, None, :, None]).reshape(elem_count, levels, width)


def solution(mesh):
    placed = (P("elem", "lev", None), P("elem", None), P("elem", None, None), P("elem"), P())
    return jax.shard_map(
        per_device, mesh=mesh, in_specs=placed, out_specs=P("elem", "lev", None), check_vma=False
    )
```

profile of v0, /device:TPU:0, one launch (start us, length us, event | category | flops | bytes accessed | tf_op | source)
XLA Modules:
  0.0 54.3 jit_solution(1006085163537011619)
XLA Ops:
  0.0 0.0 copy-start
  0.0 4.5 %collective-permute-start.1 = (f32[64,4,640]{2,1,0:T(4,128)}, f32[64,4,640]{2,1,0:T(4,128)S(1)}, u32[]{:S(2)}, u32[]{:S(2)}) collective-permute-start(f32[64,4,640]{2,1,0:T(4,128)} %param.6), channel_id=1, source_target_pairs={{4,0},{8,4},{12,8},{16,12},{20,16},{24,20},{28,24},{0,28},{5,1},{9... | collective-permute-start | bytes 1966088 | tf_op jit(solution)/shard_map/ppermute | solution.py:20
  4.5 0.0 collective-permute-start
  4.6 0.8 %maximum_bitcast_fusion = (s32[16]{0:T(128)S(1)}, s32[16]{0:T(128)S(1)}) fusion(s32[1,2,16]{2,1,0:T(2,128)} %param.8), kind=kLoop, calls=%fused_computation.29 | loop fusion | flops 48 | bytes 256 | tf_op jit(solution)/shard_map/max | solution.py:65
  5.3 0.1 broadcast_multiply_fusion
  5.4 0.1 reshape.146
  5.5 1.5 %fusion.1 = f32[64,16,16]{0,2,1:T(8,128)S(1)} fusion(f32[64,16,1]{0,1,2:T(8,128)S(1)} %reshape.146, s32[64,16]{0,1:T(8,128)} %param.7), kind=kOutput, calls=%fused_computation.8 | convolution fusion | flops 12648448 | bytes 73728 | tf_op jit(solution)/shard_map/epr,rn->epn/dot_general | solution.py:52
  7.0 1.0 %copy.23 = f32[64,16,16]{2,1,0:T(8,128)} copy(f32[64,16,16]{0,2,1:T(8,128)S(1)} %fusion.1) | data formatting | bytes 131072 | tf_op jit(solution)/shard_map/epr,rn->epn/dot_general | solution.py:52
  8.0 0.8 %broadcast_multiply_fusion.1 = f32[4,4]{1,0:T(4,128)S(1)} fusion(f32[4]{0:T(128)} %constant.76.clone), kind=kLoop, calls=%fused_computation.16 | loop fusion | flops 16 | bytes 80 | tf_op jit(solution)/shard_map/mul | solution.py:44
  8.8 0.1 reshape.147
  8.9 0.1 pad_add_fusion
  9.0 0.7 %compare_select_fusion.1 = s32[64]{0:T(128)S(1)} fusion(s32[64]{0:T(128)} %param.9), kind=kLoop, calls=%fused_computation.14 | loop fusion | flops 192 | bytes 512 | tf_op jit(solution)/shard_map/select_n | solution.py:68
  9.6 0.8 %gather_fusion = s32[64]{0:T(128)S(1)} fusion(s32[96]{0:T(128)S(1)} %pad_add_fusion, s32[1024]{0:T(1024)S(1)} %pad_clamp_fusion.1), kind=kCustom, calls=%fused_computation | custom fusion | bytes 768 | tf_op jit(solution)/shard_map/gather | solution.py:68
  10.4 7.6 %collective-permute-done.1 = f32[64,4,640]{2,1,0:T(4,128)S(1)} collective-permute-done((f32[64,4,640]{2,1,0:T(4,128)}, f32[64,4,640]{2,1,0:T(4,128)S(1)}, u32[]{:S(2)}, u32[]{:S(2)}) %collective-permute-start.1) | collective-permute-done | bytes 655392 | tf_op jit(solution)/shard_map/ppermute | solution.py:20
  18.0 3.0 %collective-permute-done = f32[64,4,640]{2,1,0:T(4,128)} collective-permute-done((f32[64,4,640]{2,1,0:T(4,128)}, f32[64,4,640]{2,1,0:T(4,128)}, u32[]{:S(2)}, u32[]{:S(2)}) %collective-permute-start) | collective-permute-done | bytes 655392 | tf_op jit(solution)/shard_map/ppermute | solution.py:18
  21.1 0.0 copy-done
  21.1 1.5 %pad_maximum_fusion = f32[192,4,640]{2,1,0:T(4,128)S(1)} fusion(f32[64,4,640]{2,1,0:T(4,128)S(1)} %collective-permute-done.1, f32[64,4,640]{2,1,0:T(4,128)S(1)} %copy-done, f32[64,4,640]{2,1,0:T(4,128)} %collective-permute-done), kind=kLoop, calls=%fused_computation.2 | loop fusion | flops 983040 | bytes 3932160 | tf_op jit(solution)/shard_map/concatenate | solution.py:16
  22.6 1.0 %gather_fusion.1 = f32[64,4,640]{2,1,0:T(4,128)S(1)} fusion(f32[192,4,640]{2,1,0:T(4,128)S(1)} %pad_maximum_fusion, s32[1024]{0:T(1024)S(1)} %pad_clamp_fusion), kind=kCustom, calls=%fused_computation.1 | custom fusion | bytes 1310976 | tf_op jit(solution)/shard_map/gather | solution.py:68
  23.5 0.4 copy.21
  24.0 0.5 fusion.7
  24.5 1.1 %copy.22 = f32[64,160,16]{1,2,0:T(8,128)S(1)} copy(f32[64,160,16]{0,2,1:T(8,128)S(1)} %bitcast.26) | data formatting | bytes 1310720 | tf_op jit(solution)/shard_map/reshape | solution.py:53
  25.6 0.0 copy-start.1
  25.6 0.1 copy.25
  25.7 0.1 copy.24
  25.8 2.1 %fusion.8 = (f32[160,16]{0,1:T(8,128)S(1)}, f32[64,160,16]{1,2,0:T(8,128)S(1)}) fusion(f32[64,160]{1,0:T(8,128)S(1)} %copy.25, f32[64,160]{1,0:T(8,128)S(1)} %copy.24, f32[64,160,16]{1,2,0:T(8,128)S(1)} %copy.22, f32[64,16,16]{2,1,0:T(8,128)} %copy.23), kind=kOutput, calls=%fused_computation.32 | convolution fusion | flops 31946240 | bytes 1468416 | tf_op jit(solution)/shard_map/epn,ecn->ecp/dot_general | solution.py:54
  28.0 0.1 reduce_sum.14
  28.1 0.1 convolution_bitcast_fusion
  28.2 9.9 %psum.14 = f32[40]{0:T(128)S(1)} all-reduce(f32[40]{0:T(128)S(1)} %convolution_bitcast_fusion), channel_id=1, replica_groups=mesh['elem'=8,'lev'=4] {'lev'}, use_global_device_ids=true, to_apply=%region_4.0 | all-reduce | flops 40 | bytes 320 | tf_op jit(solution)/shard_map/psum | solution.py:73
  38.1 13.6 %psum.15 = f32[40]{0:T(128)S(1)} all-reduce(f32[40]{0:T(128)S(1)} %psum.14), channel_id=1, replica_groups=mesh['elem'=8,'lev'=4] {'elem'}, use_global_device_ids=true, to_apply=%region_5.6 | all-reduce | flops 40 | bytes 320 | tf_op jit(solution)/shard_map/psum | solution.py:74
  51.7 0.0 copy-done.1
  51.7 0.1 mul.156
  51.8 0.1 mul.157
  51.8 1.1 %copy.26 = f32[64,160,16]{0,2,1:T(8,128)S(1)} copy(f32[64,160,16]{1,2,0:T(8,128)S(1)} %get-tuple-element.10) | data formatting | bytes 1310720 | tf_op jit(solution)/shard_map/min | solution.py:57
  52.9 0.2 bitcast_multiply_fusion
  53.1 1.2 %copy.27 = f32[64,4,640]{2,1,0:T(4,128)} copy(f32[64,4,640]{0,2,1:T(8,128)S(1)} %bitcast_multiply_fusion) | data formatting | bytes 1310720 | tf_op jit(solution)/shard_map/mul | solution.py:77
  (9 shorter events, 0.1 us)
Async XLA Ops:
  0.0 21.1 %copy-start = (f32[64,4,640]{2,1,0:T(4,128)S(1)}, f32[64,4,640]{2,1,0:T(4,128)}, u32[]{:S(2)}) copy-start(f32[64,4,640]{2,1,0:T(4,128)} %param.6) | copy-start | bytes 1966084
  0.0 18.0 %collective-permute-start.1 = (f32[64,4,640]{2,1,0:T(4,128)}, f32[64,4,640]{2,1,0:T(4,128)S(1)}, u32[]{:S(2)}, u32[]{:S(2)}) collective-permute-start(f32[64,4,640]{2,1,0:T(4,128)} %param.6), channel_id=1, source_target_pairs={{4,0},{8,4},{12,8},{16,12},{20,16},{24,20},{28,24},{0,28},{5,1},{9... | collective-permute-start | bytes 1966088 | tf_op jit(solution)/shard_map/ppermute | solution.py:20
  4.5 16.5 %collective-permute-start = (f32[64,4,640]{2,1,0:T(4,128)}, f32[64,4,640]{2,1,0:T(4,128)}, u32[]{:S(2)}, u32[]{:S(2)}) collective-permute-start(f32[64,4,640]{2,1,0:T(4,128)} %param.6), channel_id=1, source_target_pairs={{0,4},{4,8},{8,12},{12,16},{16,20},{20,24},{24,28},{28,0},{1,5},{5... | collective-permute-start | bytes 1966088 | tf_op jit(solution)/shard_map/ppermute | solution.py:18
  25.6 26.1 %copy-start.1 = (f32[40]{0:T(128)S(1)}, f32[40]{0:T(128)}, u32[]{:S(2)}) copy-start(f32[40]{0:T(128)} %param.10) | copy-start | bytes 484
where the time goes:
time: 54.6 us; the launch traced here: 54.3 us
  blocking collectives  23.5 us (43%)
  waiting for transfers between devices  10.6 us (19%)
  local copies, waits for them, and re-layouts  7.18 us (13%)
  other arithmetic  4.66 us (9%)
  starting transfers between devices  4.52 us (8%)
  matrix products  3.75 us (7%)
    psum x1, blocking collectives, per_device(): global_mass = lax.psum(column_mass, 'elem')  13.6 us
    psum x1, blocking collectives, per_device(): column_mass = lax.psum(local_mass, 'lev')  9.89 us
    ppermute x1, waiting for transfers between devices, with_halo(): lax.ppermute(head, axis, [((i + 1) % count, i) for i in range(count)])  7.59 us
    ppermute x1, starting transfers between devices, with_halo(): lax.ppermute(head, axis, [((i + 1) % count, i) for i in range(count)])  4.52 us
    ppermute x1, waiting for transfers between devices, with_halo(): lax.ppermute(tail, axis, [(i, (i + 1) % count) for i in range(count)])  3.03 us
    gather x3, local copies, waits for them, and re-layouts, per_device(): source_rows = beside_all[slot_pos[source]]  2.17 us
    dot_general x1, matrix products, interpolate(): jnp.einsum('epn,ecn->ecp', matrix, values, precision=lax.Precision.HIGHEST)  2.15 us
    concatenate x1, other arithmetic, with_halo(): jnp.concatenate([lax.ppermute(tail, axis, [(i, (i + 1) % count) for i in...  1.51 us
  transfers between devices with their start and end apart: 2, of which 2 were waited for; matrix products, arithmetic and copies ran while one was open for 11% of the time, Pallas kernels for 0%

commit v1 on v0

--- a/solution.py
+++ b/solution.py
@@ -71,7 +71,8 @@
     shaped = clipped.reshape(elem_count, levels, tracer_count, NPTS)
     local_mass = jnp.einsum("eltn,n->t", shaped, quadrature(), precision=lax.Precision.HIGHEST)
     column_mass = lax.psum(local_mass, "lev")
-    global_mass = lax.psum(column_mass, "elem")
+    terms = lax.all_gather(column_mass, "elem")
+    global_mass = jnp.sum(terms, axis=0)
     whole_weight = 4.0 * elem_count * lax.axis_size("elem") * levels * lax.axis_size("lev")
     factor = target_mean * whole_weight / global_mass
     return (shaped * factor[None, None, :, None]).reshape(elem_count, levels, width)

time: 54.6 us -> 50.8 us (0.930)
  blocking collectives: 23.5 us -> 19.7 us
    psum x1 -> x0, blocking collectives: 13.6 us -> none  [per_device(): global_mass = lax.psum(column_mass, 'elem')]
    all_gather x0 -> x1, blocking collectives: none -> 9.8 us  [per_device(): terms = lax.all_gather(column_mass, 'elem')]
  transfers between devices with their start and end apart: 2 -> 2, of which waited for: 2 -> 2; matrix products, arithmetic and copies ran while one was open for 11% -> 12% of each run, Pallas kernels for 0% -> 0%
where the time goes in v1:
time: 50.8 us; the launch traced here: 50.6 us
  blocking collectives  19.7 us (39%)
  waiting for transfers between devices  10.6 us (21%)
  local copies, waits for them, and re-layouts  7.18 us (14%)
  other arithmetic  4.69 us (9%)
  starting transfers between devices  4.52 us (9%)
  matrix products  3.75 us (7%)
    psum x1, blocking collectives, per_device(): column_mass = lax.psum(local_mass, 'lev')  9.89 us
    all_gather x1, blocking collectives, per_device(): terms = lax.all_gather(column_mass, 'elem')  9.8 us
    ppermute x1, waiting for transfers between devices, with_halo(): lax.ppermute(head, axis, [((i + 1) % count, i) for i in range(count)])  7.59 us
    ppermute x1, starting transfers between devices, with_halo(): lax.ppermute(head, axis, [((i + 1) % count, i) for i in range(count)])  4.52 us
    ppermute x1, waiting for transfers between devices, with_halo(): lax.ppermute(tail, axis, [(i, (i + 1) % count) for i in range(count)])  3.03 us
    gather x3, local copies, waits for them, and re-layouts, per_device(): source_rows = beside_all[slot_pos[source]]  2.17 us
    dot_general x1, matrix products, interpolate(): jnp.einsum('epn,ecn->ecp', matrix, values, precision=lax.Precision.HIGHEST)  2.15 us
    concatenate x1, other arithmetic, with_halo(): jnp.concatenate([lax.ppermute(tail, axis, [(i, (i + 1) % count) for i in...  1.51 us
  transfers between devices with their start and end apart: 2, of which 2 were waited for; matrix products, arithmetic and copies ran while one was open for 12% of the time, Pallas kernels for 0%

profile of v1, /device:TPU:0, one launch (start us, length us, event | category | flops | bytes accessed | tf_op | source)
XLA Modules:
  0.0 50.6 jit_solution(4275211021458498185)
XLA Ops:
  0.0 0.0 copy-start
  0.0 4.5 %collective-permute-start.1 = (f32[64,4,640]{2,1,0:T(4,128)}, f32[64,4,640]{2,1,0:T(4,128)S(1)}, u32[]{:S(2)}, u32[]{:S(2)}) collective-permute-start(f32[64,4,640]{2,1,0:T(4,128)} %param.6), channel_id=1, source_target_pairs={{4,0},{8,4},{12,8},{16,12},{20,16},{24,20},{28,24},{0,28},{5,1},{9... | collective-permute-start | bytes 1966088 | tf_op jit(solution)/shard_map/ppermute | solution.py:20
  4.5 0.0 collective-permute-start
  4.6 0.8 %maximum_bitcast_fusion = (s32[16]{0:T(128)S(1)}, s32[16]{0:T(128)S(1)}) fusion(s32[1,2,16]{2,1,0:T(2,128)} %param.8), kind=kLoop, calls=%fused_computation.28 | loop fusion | flops 48 | bytes 256 | tf_op jit(solution)/shard_map/max | solution.py:65
  5.3 0.1 broadcast_multiply_fusion
  5.4 0.1 reshape.148
  5.5 1.5 %fusion.1 = f32[64,16,16]{0,2,1:T(8,128)S(1)} fusion(f32[64,16,1]{0,1,2:T(8,128)S(1)} %reshape.148, s32[64,16]{0,1:T(8,128)} %param.7), kind=kOutput, calls=%fused_computation.7 | convolution fusion | flops 12648448 | bytes 73728 | tf_op jit(solution)/shard_map/epr,rn->epn/dot_general | solution.py:52
  7.0 1.0 %copy.23 = f32[64,16,16]{2,1,0:T(8,128)} copy(f32[64,16,16]{0,2,1:T(8,128)S(1)} %fusion.1) | data formatting | bytes 131072 | tf_op jit(solution)/shard_map/epr,rn->epn/dot_general | solution.py:52
  8.0 0.8 %broadcast_multiply_fusion.1 = f32[4,4]{1,0:T(4,128)S(1)} fusion(f32[4]{0:T(128)} %constant.76.clone), kind=kLoop, calls=%fused_computation.15 | loop fusion | flops 16 | bytes 80 | tf_op jit(solution)/shard_map/mul | solution.py:44
  8.8 0.1 reshape.149
  8.9 0.1 pad_add_fusion
  9.0 0.7 %compare_select_fusion.1 = s32[64]{0:T(128)S(1)} fusion(s32[64]{0:T(128)} %param.9), kind=kLoop, calls=%fused_computation.13 | loop fusion | flops 192 | bytes 512 | tf_op jit(solution)/shard_map/select_n | solution.py:68
  9.6 0.8 %gather_fusion = s32[64]{0:T(128)S(1)} fusion(s32[96]{0:T(128)S(1)} %pad_add_fusion, s32[1024]{0:T(1024)S(1)} %pad_clamp_fusion.1), kind=kCustom, calls=%fused_computation | custom fusion | bytes 768 | tf_op jit(solution)/shard_map/gather | solution.py:68
  10.4 7.6 %collective-permute-done.1 = f32[64,4,640]{2,1,0:T(4,128)S(1)} collective-permute-done((f32[64,4,640]{2,1,0:T(4,128)}, f32[64,4,640]{2,1,0:T(4,128)S(1)}, u32[]{:S(2)}, u32[]{:S(2)}) %collective-permute-start.1) | collective-permute-done | bytes 655392 | tf_op jit(solution)/shard_map/ppermute | solution.py:20
  18.0 3.0 %collective-permute-done = f32[64,4,640]{2,1,0:T(4,128)} collective-permute-done((f32[64,4,640]{2,1,0:T(4,128)}, f32[64,4,640]{2,1,0:T(4,128)}, u32[]{:S(2)}, u32[]{:S(2)}) %collective-permute-start) | collective-permute-done | bytes 655392 | tf_op jit(solution)/shard_map/ppermute | solution.py:18
  21.1 0.0 copy-done
  21.1 1.5 %pad_maximum_fusion = f32[192,4,640]{2,1,0:T(4,128)S(1)} fusion(f32[64,4,640]{2,1,0:T(4,128)S(1)} %collective-permute-done.1, f32[64,4,640]{2,1,0:T(4,128)S(1)} %copy-done, f32[64,4,640]{2,1,0:T(4,128)} %collective-permute-done), kind=kLoop, calls=%fused_computation.2 | loop fusion | flops 983040 | bytes 3932160 | tf_op jit(solution)/shard_map/concatenate | solution.py:16
  22.6 1.0 %gather_fusion.1 = f32[64,4,640]{2,1,0:T(4,128)S(1)} fusion(f32[192,4,640]{2,1,0:T(4,128)S(1)} %pad_maximum_fusion, s32[1024]{0:T(1024)S(1)} %pad_clamp_fusion), kind=kCustom, calls=%fused_computation.1 | custom fusion | bytes 1310976 | tf_op jit(solution)/shard_map/gather | solution.py:68
  23.5 0.4 copy.21
  24.0 0.5 %fusion.7 = (f32[64,160]{0,1:T(8,128)S(1)}, f32[64,160]{0,1:T(8,128)S(1)}) fusion(f32[64,160,16]{0,2,1:T(8,128)S(1)} %bitcast.25), kind=kLoop, calls=%fused_computation.30 | loop fusion | flops 307200 | bytes 737280 | tf_op jit(solution)/shard_map/reduce_min | solution.py:55
  24.5 1.1 %copy.22 = f32[64,160,16]{1,2,0:T(8,128)S(1)} copy(f32[64,160,16]{0,2,1:T(8,128)S(1)} %bitcast.26) | data formatting | bytes 1310720 | tf_op jit(solution)/shard_map/reshape | solution.py:53
  25.6 0.0 copy-start.1
  25.6 0.1 copy.25
  25.7 0.1 copy.24
  25.8 2.1 %fusion.8 = (f32[160,16]{0,1:T(8,128)S(1)}, f32[64,160,16]{1,2,0:T(8,128)S(1)}) fusion(f32[64,160]{1,0:T(8,128)S(1)} %copy.25, f32[64,160]{1,0:T(8,128)S(1)} %copy.24, f32[64,160,16]{1,2,0:T(8,128)S(1)} %copy.22, f32[64,16,16]{2,1,0:T(8,128)} %copy.23), kind=kOutput, calls=%fused_computation.31 | convolution fusion | flops 31946240 | bytes 1468416 | tf_op jit(solution)/shard_map/epn,ecn->ecp/dot_general | solution.py:54
  28.0 0.1 reduce_sum.26
  28.1 0.1 fusion.9
  28.2 9.9 %psum.7 = f32[1,40]{1,0:T(1,128)S(1)} all-reduce(f32[1,40]{1,0:T(1,128)S(1)} %fusion.9), channel_id=1, replica_groups=mesh['elem'=8,'lev'=4] {'lev'}, use_global_device_ids=true, to_apply=%region_4.0 | all-reduce | flops 40 | bytes 320 | tf_op jit(solution)/shard_map/psum | solution.py:73
  38.1 9.8 %all-gather = f32[8,1,40]{2,1,0:T(1,128)S(1)} all-gather(f32[1,1,40]{2,1,0:T(1,128)S(1)} %bitcast.28), channel_id=1, replica_groups=mesh['elem'=8,'lev'=4] {'elem'}, dimensions={0}, use_global_device_ids=true | all-gather | bytes 1440 | tf_op jit(solution)/shard_map/all_gather | solution.py:74
  47.9 0.0 copy-done.1
  47.9 0.1 mul.156
  48.0 0.1 mul.157
  48.1 1.1 %copy.26 = f32[64,160,16]{0,2,1:T(8,128)S(1)} copy(f32[64,160,16]{1,2,0:T(8,128)S(1)} %get-tuple-element.10) | data formatting | bytes 1310720 | tf_op jit(solution)/shard_map/min | solution.py:57
  49.2 0.2 bitcast_multiply_fusion
  49.3 1.2 %copy.27 = f32[64,4,640]{2,1,0:T(4,128)} copy(f32[64,4,640]{0,2,1:T(8,128)S(1)} %bitcast_multiply_fusion) | data formatting | bytes 1310720 | tf_op jit(solution)/shard_map/mul | solution.py:78
  (10 shorter events, 0.1 us)
Async XLA Ops:
  0.0 21.1 %copy-start = (f32[64,4,640]{2,1,0:T(4,128)S(1)}, f32[64,4,640]{2,1,0:T(4,128)}, u32[]{:S(2)}) copy-start(f32[64,4,640]{2,1,0:T(4,128)} %param.6) | copy-start | bytes 1966084
  0.0 18.0 %collective-permute-start.1 = (f32[64,4,640]{2,1,0:T(4,128)}, f32[64,4,640]{2,1,0:T(4,128)S(1)}, u32[]{:S(2)}, u32[]{:S(2)}) collective-permute-start(f32[64,4,640]{2,1,0:T(4,128)} %param.6), channel_id=1, source_target_pairs={{4,0},{8,4},{12,8},{16,12},{20,16},{24,20},{28,24},{0,28},{5,1},{9... | collective-permute-start | bytes 1966088 | tf_op jit(solution)/shard_map/ppermute | solution.py:20
  4.5 16.5 %collective-permute-start = (f32[64,4,640]{2,1,0:T(4,128)}, f32[64,4,640]{2,1,0:T(4,128)}, u32[]{:S(2)}, u32[]{:S(2)}) collective-permute-start(f32[64,4,640]{2,1,0:T(4,128)} %param.6), channel_id=1, source_target_pairs={{0,4},{4,8},{8,12},{12,16},{16,20},{20,24},{24,28},{28,0},{1,5},{5... | collective-permute-start | bytes 1966088 | tf_op jit(solution)/shard_map/ppermute | solution.py:18
  25.6 22.3 %copy-start.1 = (f32[40]{0:T(128)S(1)}, f32[40]{0:T(128)}, u32[]{:S(2)}) copy-start(f32[40]{0:T(128)} %param.10) | copy-start | bytes 484
